TPU v7x, 128 devices: a whole 4x4x4 slice. The times are simulated.
128 devices in a mesh: row: 8 (over y_hi, x), col: 16 (over y_lo, z, core).
Axes of the slice: x: 4, y: 4 (y_hi: 2, y_lo: 2; y = y_hi * 2 + y_lo), z: 4, core: 2. Of those that a mesh axis runs over, the one named last changes fastest.
Arguments:
- front_matrix: float32 [8, 8, 256, 4, 16, 256], P(None, 'row', None, None, 'col'), may hold values from -6 to 6
- swap_rows: int32 [3, 256], replicated, may hold values from 0 to 16383, as said below
- l_inverse: float32 [3, 256, 256], replicated, may hold values from -1 to 1, as said below
- u_inverse: float32 [3, 256, 256], replicated, may hold values from -1 to 1, as said below
- contrib_tiles: float32 [12288, 128, 128], P(('row', 'col')), may hold values from -6 to 6
- tile_owner: int32 [12288, 1], P(('row', 'col')), may hold values from 0 to 127; in each aligned block of 96 rows (0 to 95, 96 to 191, ...) at most 2 rows name the same one
- tile_spot: int32 [12288], P(('row', 'col')), may hold values from 0 to 127
Outputs:
- factored: float32 [8, 8, 256, 4, 16, 256], P(None, 'row', None, None, 'col')
Inputs may be any that keep to these rules, and one draw needn't show every extreme that they name: For every k and j, swap_rows[k, j] is either k * 256 + j or a row of (k + 1) * 256 or more; within one k the entries of the second kind are distinct. Each l_inverse[k] is unit lower triangular. Each u_inverse[k] is upper triangular with a positive diagonal. `tile_owner`: among the 96 tiles held by one device, at most 2 have the same owner; some device's tiles reach that bound.
All inputs are finite; a program needn't handle non-finite values.
Results may differ from a plain program's by a relative error of at most 0.00015.
Values sent between devices are 32-bit elements; how exact they have to be, the bound alone decides.
No kernel may reach another device: no remote copies, remote signals or barrier semaphores. Data moves between devices by JAX's collectives and lax.ppermute only.
A program may use at most 192 MiB of HBM per device.

v0:
```python
import jax
import jax.numpy as jnp
from jax import lax
from jax.sharding import PartitionSpec as P

STEPS = 3
CAP = 2


def packed_total(arrays, axis):
    ends = [0]
    for a in arrays:
        ends.append(ends[-1] + a.size)
    running = lax.psum(jnp.concatenate([a.ravel() for a in arrays]), axis)
    return tuple((running[b:e].reshape(a.shape) for a, b, e in zip(arrays, ends, ends[1:])))


def padded_to(lines, count):
    spare = -lines.shape[0] % count
    if not spare:
        return lines
    return jnp.concatenate([lines, jnp.zeros((spare, *lines.shape[1:]), lines.dtype)])


def broadcast_by_parts(value, axis, root):
    lines = jnp.where(lax.axis_index(axis) == root, value, jnp.zeros_like(value)).reshape(
        -1, *value.shape[1:][-1:]
    )
    padded = padded_to(lines, lax.axis_size(axis))
    own = lax.psum_scatter(padded, axis, scatter_dimension=0, tiled=True)
    return lax.all_gather(own, axis, axis=0, tiled=True)[: len(lines)].reshape(value.shape)


def deliver(contrib_tiles, tile_owner, tile_spot):
    tile_count, tile_edge, unused_edge = contrib_tiles.shape
    row_count = lax.axis_size("row")
    col_count = lax.axis_size("col")
    devices = row_count * col_count
    owners = tile_owner[:, 0]
    matches = (owners[:, None] == jnp.arange(devices, dtype=jnp.int32)[None, :]).astype(jnp.int32)
    slot_rank = jnp.sum((jnp.cumsum(matches, axis=0) - matches) * matches, axis=1)
    slot_index = owners * CAP + slot_rank
    flat_tiles = contrib_tiles.reshape(tile_count, tile_edge * tile_edge)
    sending = (
        jnp.zeros((devices * CAP, tile_edge * tile_edge), jnp.float32)
        .at[slot_index]
        .set(flat_tiles)
    )
    spot_ids = jnp.full((devices * CAP,), -1, jnp.int32).at[slot_index].set(tile_spot)
    received, spot_in = (
        lax.all_to_all(
            sending.reshape(devices, CAP, tile_edge * tile_edge),
            ("row", "col"),
            split_axis=0,
            concat_axis=0,
            tiled=True,
        ),
        lax.all_to_all(
            spot_ids.reshape(devices, CAP), ("row", "col"), split_axis=0, concat_axis=0, tiled=True
        ),
    )
    return (received.reshape(devices * CAP, tile_edge * tile_edge), spot_in.reshape(devices * CAP))


def assemble(matrix, received, spot_in, tile_edge):
    local_rows, local_cols = matrix.shape
    row_tiles = local_rows // tile_edge
    col_tiles = local_cols // tile_edge
    onehot = (
        spot_in[None, :] == jnp.arange(row_tiles * col_tiles, dtype=jnp.int32)[:, None]
    ).astype(jnp.float32)
    assembled = jnp.dot(
        onehot, received, precision=lax.Precision.HIGHEST, preferred_element_type=jnp.float32
    )
    assembled = (
        assembled.reshape(row_tiles, col_tiles, tile_edge, tile_edge)
        .transpose(0, 2, 1, 3)
        .reshape(local_rows, local_cols)
    )
    return matrix + assembled


def local(front_matrix, swap_rows, l_inverse, u_inverse, contrib_tiles, tile_owner, tile_spot):
    precise = lax.Precision.HIGHEST
    block_rows, unused_row, block_width, block_cols, unused_col, unused_width = front_matrix.shape
    row_count = lax.axis_size("row")
    col_count = lax.axis_size("col")
    row_place = lax.axis_index("row")
    col_place = lax.axis_index("col")
    local_rows = block_rows * block_width
    local_cols = block_cols * block_width
    matrix = front_matrix.reshape(local_rows, local_cols)
    index_rows = jnp.arange(local_rows, dtype=jnp.int32)
    index_cols = jnp.arange(local_cols, dtype=jnp.int32)
    global_rows = (
        index_rows // block_width * row_count + row_place
    ) * block_width + index_rows % block_width
    global_cols = (
        index_cols // block_width * col_count + col_place
    ) * block_width + index_cols % block_width
    for window_step in range(STEPS):
        past_row = (window_step + 1) * block_width
        targets = swap_rows[window_step]
        home_block = targets // block_width
        owned_here = home_block % row_count == row_place
        local_index = home_block // row_count * block_width + targets % block_width
        top_root = window_step % row_count
        top_start = window_step // row_count * block_width
        top_slab = matrix[top_start : top_start + block_width]
        picked = jnp.where(owned_here[:, None], matrix[jnp.where(owned_here, local_index, 0)], 0.0)
        top_part = jnp.where(row_place == top_root, top_slab, 0.0)
        chosen, leaving = packed_total((picked, top_part), "row")
        landing = jnp.where(owned_here, local_index, local_rows)
        matrix = matrix.at[landing].set(leaving, mode="drop")
        current_top = matrix[top_start : top_start + block_width]
        matrix = matrix.at[top_start : top_start + block_width].set(
            jnp.where(row_place == top_root, chosen, current_top)
        )
        panel_root = window_step % col_count
        panel_start = window_step // col_count * block_width
        below_mask = (global_rows >= past_row)[:, None]
        right_mask = (global_cols >= past_row)[None, :]
        panel_slab = matrix[:, panel_start : panel_start + block_width]
        lower_part = jnp.where(
            below_mask,
            jnp.dot(
                panel_slab,
                u_inverse[window_step],
                precision=precise,
                preferred_element_type=jnp.float32,
            ),
            0.0,
        )
        lower_part = broadcast_by_parts(lower_part, "col", panel_root)
        upper_part = jnp.where(
            right_mask,
            jnp.dot(
                l_inverse[window_step],
                chosen,
                precision=precise,
                preferred_element_type=jnp.float32,
            ),
            0.0,
        )
        matrix = matrix.at[:, panel_start : panel_start + block_width].set(
            jnp.where(below_mask & (col_place == panel_root), lower_part, panel_slab)
        )
        current_top = matrix[top_start : top_start + block_width]
        matrix = matrix.at[top_start : top_start + block_width].set(
            jnp.where(right_mask & (row_place == top_root), upper_part, current_top)
        )
        matrix = matrix - jnp.dot(
            lower_part, upper_part, precision=precise, preferred_element_type=jnp.float32
        )
    received, spot_in = deliver(contrib_tiles, tile_owner, tile_spot)
    matrix = assemble(matrix, received, spot_in, contrib_tiles.shape[1])
    return matrix.reshape(front_matrix.shape)


def solution(mesh):
    placed = (
        P(None, "row", None, None, "col", None),
        P(),
        P(),
        P(),
        P(("row", "col"), None, None),
        P(("row", "col"), None),
        P(("row", "col")),
    )
    return jax.shard_map(
        local,
        mesh=mesh,
        in_specs=placed,
        out_specs=P(None, "row", None, None, "col", None),
        check_vma=False,
    )
```

profile of v0, /device:TPU:30, one launch (start us, length us, event | category | flops | bytes accessed | tf_op | source)
XLA Modules:
  0.0 957.2 jit_solution(2932770433654854582)
XLA Ops:
  8.2 26.7 %reduce.23 = f32[8,256,4,256]{3,2,1,0:T(4,128)} reduce(f32[8,1,256,4,1,256]{5,4,3,2,1,0:T(1,128)} %param.25, f32[]{:T(128)} %constant.395), dimensions={1,4}, to_apply=%param.25.reduce_sub_computation | reduce | bytes 16777220 | tf_op args[0]
  34.9 8.7 copy.27
  52.6 92.6 %all-reduce.4.cloned.1.call-done = f32[524288]{0:T(1024)} async-done(((f32[524288]{0:T(1024)}), f32[524288]{0:T(1024)}) %all-reduce.4.cloned.1.call-update) | async-done | bytes 2097168 | tf_op jit(solution)/shard_map/psum | solution.py:14
  147.3 8.2 scatter_fusion
  162.6 64.9 %reduce-scatter.4.cloned.1.call-done = f32[128,256]{1,0:T(8,128)} async-done(((f32[2048,256]{1,0:T(8,128)}), f32[128,256]{1,0:T(8,128)}) %reduce-scatter.4.cloned.1.call-update) | async-done | bytes 131088 | tf_op jit(solution)/shard_map/reduce_scatter | solution.py:30
  228.3 33.5 %all-gather.4.cloned.1.call-done = f32[2048,256]{1,0:T(8,128)} async-done(((f32[128,256]{1,0:T(8,128)}), f32[2048,256]{1,0:T(8,128)}) %all-gather.4.cloned.1.call-update) | async-done | bytes 2097168 | tf_op jit(solution)/shard_map/all_gather | solution.py:31
  269.5 9.8 %convolution_subtract_fusion.1 = f32[2048,1024]{1,0:T(8,128)S(1)} fusion(f32[2048,1024]{1,0:T(8,128)} %get-tuple-element.141, f32[2048,256]{1,0:T(8,128)S(1)} %copy-done.5, f32[1024,256]{0,1:T(8,128)S(1)} %get-tuple-element.142), kind=kOutput, calls=%fused_computation.14 | convolution fusion | flops 6444548096 | bytes 19922944 | tf_op jit(solution)/shard_map/dot_general | solution.py:152
  289.9 90.9 %all-reduce.6.cloned.1.call-done = f32[524288]{0:T(1024)} async-done(((f32[524288]{0:T(1024)}), f32[524288]{0:T(1024)}) %all-reduce.6.cloned.1.call-update) | async-done | bytes 2097168 | tf_op jit(solution)/shard_map/psum | solution.py:14
  382.9 8.5 scatter_fusion.1
  398.6 64.7 %reduce-scatter.6.cloned.1.call-done = f32[128,256]{1,0:T(8,128)} async-done(((f32[2048,256]{1,0:T(8,128)}), f32[128,256]{1,0:T(8,128)}) %reduce-scatter.6.cloned.1.call-update) | async-done | bytes 131088 | tf_op jit(solution)/shard_map/reduce_scatter | solution.py:30
  463.4 34.0 %all-gather.6.cloned.1.call-done = f32[2048,256]{1,0:T(8,128)} async-done(((f32[128,256]{1,0:T(8,128)}), f32[2048,256]{1,0:T(8,128)}) %all-gather.6.cloned.1.call-update) | async-done | bytes 2097168 | tf_op jit(solution)/shard_map/all_gather | solution.py:31
  505.0 9.8 %convolution_subtract_fusion = f32[2048,1024]{1,0:T(8,128)S(1)} fusion(f32[2048,1024]{1,0:T(8,128)} %get-tuple-element.143, f32[2048,256]{1,0:T(8,128)S(1)} %copy-done.4, f32[1024,256]{0,1:T(8,128)S(1)} %get-tuple-element.144), kind=kOutput, calls=%fused_computation.13 | convolution fusion | flops 6444548096 | bytes 19922944 | tf_op jit(solution)/shard_map/dot_general | solution.py:152
  527.4 8.9 all-to-all-start
  536.3 16.6 %scatter_custom_fusion.4 = f32[256,16384]{1,0:T(8,128)} fusion(s32[96]{0:T(128)S(1)} %fusion.70, f32[]{:T(128)} %constant.384.clone.1, f32[12,8,128,128]{3,2,1,0:T(8,128)} %bitcast.136), kind=kCustom, calls=%fused_computation.9 | custom fusion | bytes 23068676 | tf_op jit(solution)/shard_map/scatter | solution.py:47
  552.9 20.1 %reshape.1077 = f32[128,2,16384]{2,1,0:T(2,128)} reshape(f32[256,16384]{1,0:T(8,128)} %scatter_custom_fusion.4) | data formatting | bytes 33554432 | tf_op jit(solution)/shard_map/reshape | solution.py:52
  573.0 10.2 %all-to-all-start.1 = ((f32[128,2,16384]{2,1,0:T(2,128)}), f32[128,2,16384]{2,1,0:T(2,128)}, u32[]{:S(2)}, u32[]{:S(2)}) async-start(f32[128,2,16384]{2,1,0:T(2,128)} %reshape.1077), calls=%async_computation.4 | async-start | bytes 33554432 | tf_op jit(solution)/shard_map/all_to_all | solution.py:51
  583.3 80.9 %all-reduce.8.cloned.1.call-done = f32[524288]{0:T(1024)} async-done(((f32[524288]{0:T(1024)}), f32[524288]{0:T(1024)}) %all-reduce.8.cloned.1.call-update) | async-done | bytes 2097168 | tf_op jit(solution)/shard_map/psum | solution.py:14
  666.2 8.0 scatter_fusion.2
  681.5 180.0 %reduce-scatter.8.cloned.1.call-done = f32[128,256]{1,0:T(8,128)} async-done(((f32[2048,256]{1,0:T(8,128)}), f32[128,256]{1,0:T(8,128)}) %reduce-scatter.8.cloned.1.call-update) | async-done | bytes 131088 | tf_op jit(solution)/shard_map/reduce_scatter | solution.py:30
  863.1 20.5 %reshape.1078 = f32[256,16384]{1,0:T(8,128)} reshape(f32[128,2,16384]{2,1,0:T(2,128)} %all-to-all-done.1) | data formatting | bytes 33554432 | tf_op jit(solution)/shard_map/reshape | solution.py:62
  883.6 17.5 %copy.21 = f32[16384,256]{1,0:T(8,128)} copy(f32[16384,256]{0,1:T(8,128)} %bitcast.132) | data formatting | bytes 33554432 | tf_op jit(solution)/shard_map/dot_general | solution.py:72
  901.2 15.0 %fusion.33 = f32[16,8,128,128]{3,1,2,0:T(8,128)} fusion(f32[128,128,256,1]{2,1,0,3:T(8,128)} %bitcast.134, s32[16,8]{1,0:T(8,128)S(1)} %multiply_add_fusion, s32[256]{0:T(256)S(1)} %eq.161), kind=kOutput, calls=%fused_computation.68 | convolution fusion | flops 6442483712 | bytes 25167360 | tf_op jit(solution)/shard_map/dot_general | solution.py:72
  924.6 12.3 %bitcast_add_fusion = f32[2048,1024]{1,0:T(8,128)} fusion(f32[256,8,8,128]{3,2,1,0:T(8,128)S(1)} %bitcast.135, f32[2048,1024]{1,0:T(8,128)} %get-tuple-element.145, f32[2048,256]{1,0:T(8,128)S(1)} %copy-done.3, f32[1024,256]{0,1:T(8,128)S(1)} %get-tuple-element.146), kind=kOutput, calls=%fused_computation.8 | convolution fusion | flops 6446645248 | bytes 28311552 | tf_op jit(solution)/shard_map/dot_general | solution.py:152
  936.8 13.5 %reshape.1147 = f32[8,1,256,4,1,256]{5,4,3,2,1,0:T(1,128)} reshape(f32[2048,1024]{1,0:T(8,128)} %bitcast_add_fusion) | data formatting | bytes 16777216 | tf_op jit(solution)/shard_map/reshape | solution.py:157
  (110 shorter events, 87.5 us)
Async XLA Ops:
  6.5 138.7 %all-reduce.4.cloned.1.call-start = ((), (), s32[]{:S(2)}) async-start(), calls=%async_computation.5 | async-start | bytes 4194304 | tf_op jit(solution)/shard_map/psum | solution.py:14
  52.5 174.9 %reduce-scatter.4.cloned.1.call-start = ((), (), s32[]{:S(2)}) async-start(), calls=%async_computation.6 | async-start | bytes 2228224 | tf_op jit(solution)/shard_map/reduce_scatter | solution.py:30
  162.5 99.2 %all-gather.4.cloned.1.call-start = ((), (), s32[]{:S(2)}) async-start(), calls=%async_computation.7 | async-start | bytes 2228224 | tf_op jit(solution)/shard_map/all_gather | solution.py:31
  227.4 153.4 %all-reduce.6.cloned.1.call-start = ((), (), s32[]{:S(2)}) async-start(), calls=%async_computation.8 | async-start | bytes 4194304 | tf_op jit(solution)/shard_map/psum | solution.py:14
  261.7 7.8 copy-start.5
  279.4 3.4 copy-start.1
  289.9 173.4 %reduce-scatter.6.cloned.1.call-start = ((), (), s32[]{:S(2)}) async-start(), calls=%async_computation.9 | async-start | bytes 2228224 | tf_op jit(solution)/shard_map/reduce_scatter | solution.py:30
  398.5 98.9 %all-gather.6.cloned.1.call-start = ((), (), s32[]{:S(2)}) async-start(), calls=%async_computation.10 | async-start | bytes 2228224 | tf_op jit(solution)/shard_map/all_gather | solution.py:31
  463.3 200.9 %all-reduce.8.cloned.1.call-start = ((), (), s32[]{:S(2)}) async-start(), calls=%async_computation.11 | async-start | bytes 4194304 | tf_op jit(solution)/shard_map/psum | solution.py:14
  497.4 7.6 copy-start.4
  514.9 3.2 copy-start
  518.4 6.8 copy-start.6
  527.4 45.6 %all-to-all-start = ((s32[128,1,2]{2,1,0:T(1,128)}), s32[128,1,2]{2,1,0:T(1,128)S(1)}, u32[]{:S(2)}, u32[]{:S(2)}) async-start(s32[128,1,2]{2,1,0:T(1,128)} %bitcast.25), calls=%async_computation.3 | async-start | bytes 131072 | tf_op jit(solution)/shard_map/all_to_all | solution.py:58
  573.0 290.1 %all-to-all-start.1 = ((f32[128,2,16384]{2,1,0:T(2,128)}), f32[128,2,16384]{2,1,0:T(2,128)}, u32[]{:S(2)}, u32[]{:S(2)}) async-start(f32[128,2,16384]{2,1,0:T(2,128)} %reshape.1077), calls=%async_computation.4 | async-start | bytes 33554432 | tf_op jit(solution)/shard_map/all_to_all | solution.py:51
  583.2 278.3 %reduce-scatter.8.cloned.1.call-start = ((), (), s32[]{:S(2)}) async-start(), calls=%async_computation.12 | async-start | bytes 2228224 | tf_op jit(solution)/shard_map/reduce_scatter | solution.py:30
  681.2 234.9 %all-gather.8.cloned.1.call-start = ((), (), s32[]{:S(2)}) async-start(), calls=%async_computation.13 | async-start | bytes 2228224 | tf_op jit(solution)/shard_map/all_gather | solution.py:31
  916.1 8.4 copy-start.2
  916.1 8.4 copy-start.3
Sparse Core Ops, SparseCore 0:
  52.6 92.5 all-reduce.3
  162.6 64.7 reduce-scatter.3
  229.1 32.5 all-gather.3
  290.0 90.8 all-reduce.5
  398.7 64.5 reduce-scatter.5
  464.8 32.5 all-gather.5
  525.3 138.8 all-reduce.7
  681.4 180.1 reduce-scatter.7
  863.3 31.6 all-gather.7
where the time goes:
time: 967 us; the launch traced here: 957 us
  waiting for transfers between devices  642 us (66%)
  local copies, waits for them, and re-layouts  153 us (16%)
  matrix products  71.8 us (7%)
  other arithmetic  56.9 us (6%)
  starting transfers between devices  19.6 us (2%)
  between operations  14 us (1%)
    reduce_scatter x3, waiting for transfers between devices, broadcast_by_parts(): own = lax.psum_scatter(padded, axis, scatter_dimension=0, tiled=True)  310 us
    psum x3, waiting for transfers between devices, packed_total(): running = lax.psum(jnp.concatenate([a.ravel() for a in arrays]), axis)  264 us
    all_gather x3, waiting for transfers between devices, broadcast_by_parts(): lax.all_gather(own, axis, axis=0, tiled=True)[:len(lines)]  67.4 us
    dot_general x3, matrix products, local(): jnp.dot(lower_part, upper_part, precision=precise, preferred_element_type...  31.9 us
    unnamed x6, other arithmetic  27.3 us
    scatter x3, local copies, waits for them, and re-layouts, local(): matrix = matrix.at[landing].set(leaving, mode='drop')  24.7 us
    reshape x1, local copies, waits for them, and re-layouts, deliver(): received.reshape(devices * CAP, tile_edge * tile_edge)  20.5 us
    reshape x1, local copies, waits for them, and re-layouts, deliver(): sending.reshape(devices, CAP, tile_edge * tile_edge)  20.1 us
  transfers between devices with their start and end apart: 11, of which 8 were waited for; matrix products, arithmetic and copies ran while one was open for 12% of the time, Pallas kernels for 0%

commit v1 on v0

--- a/solution.py
+++ b/solution.py
@@ -28,7 +28,9 @@
     )
     padded = padded_to(lines, lax.axis_size(axis))
     own = lax.psum_scatter(padded, axis, scatter_dimension=0, tiled=True)
-    return lax.all_gather(own, axis, axis=0, tiled=True)[: len(lines)].reshape(value.shape)
+    return jnp.concatenate(
+        lax.all_to_all(jnp.stack([own] * lax.axis_size(axis)), axis, 0, 0), axis=0
+    )[: len(lines)].reshape(value.shape)
 
 
 def deliver(contrib_tiles, tile_owner, tile_spot):

time: 967 us -> 1040 us (1.075)
  local copies, waits for them, and re-layouts: 153 us -> 226 us
  waiting for transfers between devices: 642 us -> 617 us
  starting transfers between devices: 19.6 us -> 34.2 us
    psum x3, waiting for transfers between devices: 264 us -> 392 us  [packed_total(): running = lax.psum(jnp.concatenate([a.ravel() for a in arrays]), axis)]
    reduce_scatter x3, waiting for transfers between devices: 310 us -> 199 us  [broadcast_by_parts(): own = lax.psum_scatter(padded, axis, scatter_dimension=0, tiled=True)]
    all_gather x3 -> x0, waiting for transfers between devices: 67.4 us -> none  [broadcast_by_parts(): lax.all_gather(own, axis, axis=0, tiled=True)[:len(lines)]]
    scatter x3 -> x6, local copies, waits for them, and re-layouts: 24.7 us -> 51.9 us  [local(): matrix = matrix.at[landing].set(leaving, mode='drop')]
    all_to_all x0 -> x3, waiting for transfers between devices: none -> 26 us  [broadcast_by_parts(): lax.all_to_all(jnp.stack([own] * lax.axis_size(axis)), axis, 0, 0)]
    sub x0 -> x2, local copies, waits for them, and re-layouts: none -> 18.5 us  [local(): matrix - jnp.dot(lower_part, upper_part, precision=precise, preferred_ele...]
    all_to_all x0 -> x3, starting transfers between devices: none -> 14.7 us  [broadcast_by_parts(): lax.all_to_all(jnp.stack([own] * lax.axis_size(axis)), axis, 0, 0)]
    unnamed x20 -> x14, local copies, waits for them, and re-layouts: 16.3 us -> 23.4 us
  transfers between devices with their start and end apart: 11 -> 11, of which waited for: 8 -> 7; matrix products, arithmetic and copies ran while one was open for 12% -> 17% of each run, Pallas kernels for 0% -> 0%
where the time goes in v1:
time: 1040 us; the launch traced here: 1030 us
  waiting for transfers between devices  617 us (59%)
  local copies, waits for them, and re-layouts  226 us (22%)
  matrix products  77.2 us (7%)
  other arithmetic  57.9 us (6%)
  starting transfers between devices  34.2 us (3%)
  between operations  14.4 us (1%)
    psum x3, waiting for transfers between devices, packed_total(): running = lax.psum(jnp.concatenate([a.ravel() for a in arrays]), axis)  392 us
    reduce_scatter x3, waiting for transfers between devices, broadcast_by_parts(): own = lax.psum_scatter(padded, axis, scatter_dimension=0, tiled=True)  199 us
    scatter x6, local copies, waits for them, and re-layouts, local(): matrix = matrix.at[landing].set(leaving, mode='drop')  51.9 us
    dot_general x3, matrix products, local(): jnp.dot(lower_part, upper_part, precision=precise, preferred_element_type...  32.3 us
    unnamed x1, other arithmetic  26.7 us
    all_to_all x3, waiting for transfers between devices, broadcast_by_parts(): lax.all_to_all(jnp.stack([own] * lax.axis_size(axis)), axis, 0, 0)  26 us
    unnamed x14, local copies, waits for them, and re-layouts  23.4 us
  transfers between devices with their start and end apart: 11, of which 7 were waited for; matrix products, arithmetic and copies ran while one was open for 17% of the time, Pallas kernels for 0%

profile of v1, /device:TPU:30, one launch (start us, length us, event | category | flops | bytes accessed | tf_op | source)
XLA Modules:
  0.0 1026.4 jit_solution(5834362631079138846)
XLA Ops:
  8.2 26.7 %reduce.23 = f32[8,256,4,256]{3,2,1,0:T(4,128)} reduce(f32[8,1,256,4,1,256]{5,4,3,2,1,0:T(1,128)} %param.25, f32[]{:T(128)} %constant.395), dimensions={1,4}, to_apply=%param.25.reduce_sub_computation | reduce | bytes 16777220 | tf_op args[0]
  53.2 92.6 %all-reduce.4.cloned.1.call-done = f32[524288]{0:T(1024)} async-done(((f32[524288]{0:T(1024)}), f32[524288]{0:T(1024)}) %all-reduce.4.cloned.1.call-update) | async-done | bytes 2097168 | tf_op jit(solution)/shard_map/psum | solution.py:14
  155.8 9.1 copy.57
  174.5 64.9 %reduce-scatter.4.cloned.1.call-done = f32[128,256]{1,0:T(8,128)} async-done(((f32[2048,256]{1,0:T(8,128)}), f32[128,256]{1,0:T(8,128)}) %reduce-scatter.4.cloned.1.call-update) | async-done | bytes 131088 | tf_op jit(solution)/shard_map/reduce_scatter | solution.py:30
  247.5 26.0 %all-to-all-done = f32[16,128,256]{1,2,0:T(8,128)S(1)} async-done(((f32[16,128,256]{1,2,0:T(8,128)}), f32[16,128,256]{1,2,0:T(8,128)S(1)}, u32[]{:S(2)}, u32[]{:S(2)}) %all-to-all-start) | async-done | bytes 2097184 | tf_op jit(solution)/shard_map/all_to_all | solution.py:32
  281.7 11.2 %convolution_subtract_fusion.1 = f32[2048,1024]{0,1:T(8,128)} fusion(f32[2048,1024]{0,1:T(8,128)} %get-tuple-element.141, f32[1024,256]{1,0:T(8,128)S(1)} %get-tuple-element.142, f32[16,128,256]{1,2,0:T(8,128)S(1)} %all-to-all-done), kind=kOutput, calls=%fused_computation.15 | convolution fusion | flops 6444548096 | bytes 19922944 | tf_op jit(solution)/shard_map/dot_general | solution.py:154
  292.9 9.3 copy.65
  311.5 93.0 %all-reduce.6.cloned.1.call-done = f32[524288]{0:T(1024)} async-done(((f32[524288]{0:T(1024)}), f32[524288]{0:T(1024)}) %all-reduce.6.cloned.1.call-update) | async-done | bytes 2097168 | tf_op jit(solution)/shard_map/psum | solution.py:14
  414.7 9.1 copy.68
  433.3 64.7 %reduce-scatter.6.cloned.1.call-done = f32[128,256]{1,0:T(8,128)} async-done(((f32[2048,256]{1,0:T(8,128)}), f32[128,256]{1,0:T(8,128)}) %reduce-scatter.6.cloned.1.call-update) | async-done | bytes 131088 | tf_op jit(solution)/shard_map/reduce_scatter | solution.py:30
  505.9 16.5 %scatter_custom_fusion.4 = f32[256,16384]{1,0:T(8,128)} fusion(s32[96]{0:T(128)S(1)} %fusion.74, f32[]{:T(128)} %constant.384.clone.1, f32[12,8,128,128]{3,2,1,0:T(8,128)} %bitcast.167), kind=kCustom, calls=%fused_computation.9 | custom fusion | bytes 23068676 | tf_op jit(solution)/shard_map/scatter | solution.py:49
  522.5 20.0 %reshape.1095 = f32[128,2,16384]{2,1,0:T(2,128)} reshape(f32[256,16384]{1,0:T(8,128)} %scatter_custom_fusion.4) | data formatting | bytes 33554432 | tf_op jit(solution)/shard_map/reshape | solution.py:54
  561.7 11.2 %convolution_subtract_fusion = f32[2048,1024]{0,1:T(8,128)} fusion(f32[2048,1024]{0,1:T(8,128)} %get-tuple-element.143, f32[1024,256]{1,0:T(8,128)S(1)} %get-tuple-element.144, f32[16,128,256]{1,2,0:T(8,128)S(1)} %all-to-all-done.1), kind=kOutput, calls=%fused_computation.14 | convolution fusion | flops 6444548096 | bytes 19922944 | tf_op jit(solution)/shard_map/dot_general | solution.py:154
  572.8 9.2 copy.76
  590.8 10.2 all-to-all-start.4
  602.7 205.9 %all-reduce.8.cloned.1.call-done = f32[524288]{0:T(1024)} async-done(((f32[524288]{0:T(1024)}), f32[524288]{0:T(1024)}) %all-reduce.8.cloned.1.call-update) | async-done | bytes 2097168 | tf_op jit(solution)/shard_map/psum | solution.py:14
  818.4 9.2 copy.79
  837.1 69.4 %reduce-scatter.8.cloned.1.call-done = f32[128,256]{1,0:T(8,128)} async-done(((f32[2048,256]{1,0:T(8,128)}), f32[128,256]{1,0:T(8,128)}) %reduce-scatter.8.cloned.1.call-update) | async-done | bytes 131088 | tf_op jit(solution)/shard_map/reduce_scatter | solution.py:30
  915.5 20.5 %reshape.1096 = f32[256,16384]{1,0:T(8,128)} reshape(f32[128,2,16384]{2,1,0:T(2,128)} %all-to-all-done.4) | data formatting | bytes 33554432 | tf_op jit(solution)/shard_map/reshape | solution.py:64
  936.0 17.5 %copy.84 = f32[16384,256]{1,0:T(8,128)} copy(f32[16384,256]{0,1:T(8,128)} %bitcast.160) | data formatting | bytes 33554432 | tf_op jit(solution)/shard_map/dot_general | solution.py:74
  953.5 12.1 %fusion.37 = f32[16,8,128,128]{3,1,2,0:T(8,128)S(1)} fusion(f32[128,128,256,1]{2,1,0,3:T(8,128)} %bitcast.165, s32[16,8]{1,0:T(8,128)S(1)} %multiply_add_fusion, s32[256]{0:T(256)S(1)} %eq.161), kind=kOutput, calls=%fused_computation.73 | convolution fusion | flops 6442483712 | bytes 25167360 | tf_op jit(solution)/shard_map/dot_general | solution.py:74
  971.1 9.2 copy.91
  988.7 10.0 subtract_add_fusion
  1006.0 13.1 %copy.86 = f32[8,1,256,4,1,256]{5,4,3,2,1,0:T(1,128)} copy(f32[8,1,256,4,1,256]{2,0,5,3,4,1:T(8,128)} %bitcast.164) | data formatting | bytes 16777216 | tf_op jit(solution)/shard_map/reshape | solution.py:159
  (122 shorter events, 171.3 us)
Async XLA Ops:
  6.5 139.3 %all-reduce.4.cloned.1.call-start = ((), (), s32[]{:S(2)}) async-start(), calls=%async_computation.8 | async-start | bytes 4194304 | tf_op jit(solution)/shard_map/psum | solution.py:14
  53.1 186.2 %reduce-scatter.4.cloned.1.call-start = ((), (), s32[]{:S(2)}) async-start(), calls=%async_computation.9 | async-start | bytes 2228224 | tf_op jit(solution)/shard_map/reduce_scatter | solution.py:30
  241.9 31.6 %all-to-all-start = ((f32[16,128,256]{1,2,0:T(8,128)}), f32[16,128,256]{1,2,0:T(8,128)S(1)}, u32[]{:S(2)}, u32[]{:S(2)}) async-start(f32[16,128,256]{1,2,0:T(8,128)} %stack.6), calls=%async_computation.1 | async-start | bytes 4194304 | tf_op jit(solution)/shard_map/all_to_all | solution.py:32
  246.7 157.8 %all-reduce.6.cloned.1.call-start = ((), (), s32[]{:S(2)}) async-start(), calls=%async_computation.10 | async-start | bytes 4194304 | tf_op jit(solution)/shard_map/psum | solution.py:14
  311.4 186.7 %reduce-scatter.6.cloned.1.call-start = ((), (), s32[]{:S(2)}) async-start(), calls=%async_computation.11 | async-start | bytes 2228224 | tf_op jit(solution)/shard_map/reduce_scatter | solution.py:30
  426.7 78.9 %copy-start.2 = (s32[96,1]{0,1:T(1,128)S(1)}, s32[96,1]{0,1:T(1,128)}, u32[]{:S(2)}) copy-start(s32[96,1]{0,1:T(1,128)} %param.30) | copy-start | bytes 1156
  500.6 43.8 %all-to-all-start.1 = ((f32[16,128,256]{1,2,0:T(8,128)}), f32[16,128,256]{1,2,0:T(8,128)S(1)}, u32[]{:S(2)}, u32[]{:S(2)}) async-start(f32[16,128,256]{1,2,0:T(8,128)} %stack.7), calls=%async_computation.3 | async-start | bytes 4194304 | tf_op jit(solution)/shard_map/all_to_all | solution.py:32
  544.4 46.4 %all-to-all-start.3 = ((s32[128,1,2]{2,1,0:T(1,128)}), s32[128,1,2]{2,1,0:T(1,128)S(1)}, u32[]{:S(2)}, u32[]{:S(2)}) async-start(s32[128,1,2]{2,1,0:T(1,128)} %bitcast.25), calls=%async_computation.6 | async-start | bytes 131072 | tf_op jit(solution)/shard_map/all_to_all | solution.py:60
  590.8 10.3 %copy-start.1 = (f32[32,8,8,128]{3,1,2,0:T(8,128)S(1)}, f32[32,8,8,128]{3,1,2,0:T(8,128)}, u32[]{:S(2)}) copy-start(f32[32,8,8,128]{3,1,2,0:T(8,128)} %copy.100) | copy-start | bytes 3145732
  590.8 316.7 %all-to-all-start.4 = ((f32[128,2,16384]{2,1,0:T(2,128)}), f32[128,2,16384]{2,1,0:T(2,128)}, u32[]{:S(2)}, u32[]{:S(2)}) async-start(f32[128,2,16384]{2,1,0:T(2,128)} %reshape.1095), calls=%async_computation.7 | async-start | bytes 33554432 | tf_op jit(solution)/shard_map/all_to_all | solution.py:53
  601.0 207.5 %all-reduce.8.cloned.1.call-start = ((), (), s32[]{:S(2)}) async-start(), calls=%async_computation.12 | async-start | bytes 4194304 | tf_op jit(solution)/shard_map/psum | solution.py:14
  602.6 303.9 %reduce-scatter.8.cloned.1.call-start = ((), (), s32[]{:S(2)}) async-start(), calls=%async_computation.13 | async-start | bytes 2228224 | tf_op jit(solution)/shard_map/reduce_scatter | solution.py:30
  909.0 71.2 %all-to-all-start.2 = ((f32[16,128,256]{1,2,0:T(8,128)}), f32[16,128,256]{1,2,0:T(8,128)S(1)}, u32[]{:S(2)}, u32[]{:S(2)}) async-start(f32[16,128,256]{1,2,0:T(8,128)} %stack.8), calls=%async_computation.5 | async-start | bytes 4194304 | tf_op jit(solution)/shard_map/all_to_all | solution.py:32
  980.2 8.5 copy-start
Sparse Core Ops, SparseCore 0:
  53.2 92.5 all-reduce.3
  174.6 64.7 reduce-scatter.3
  311.5 92.9 all-reduce.5
  433.5 64.5 reduce-scatter.5
  604.1 204.4 all-reduce.7
  837.2 69.1 reduce-scatter.7
